TPU v7x, 32 devices: a whole 2x2x4 slice. The times are simulated.
32 devices in a mesh: replica: 4 (over x, core), fsdp: 4 (over z), tensor: 2 (over y).
Axes of the slice: x: 2, y: 2, z: 4, core: 2. Of those that a mesh axis runs over, the one named last changes fastest.
Arguments:
- pseudo_grad: bfloat16 [4, 3072, 18432], P('replica', 'fsdp', 'tensor'), may hold values from -6 to 6
- compensation: float32 [4, 3072, 18432], P('replica', 'fsdp', 'tensor'), may hold values from -6 to 6
- params: float32 [3072, 18432], P(('fsdp', 'replica'), 'tensor'), may hold values from -6 to 6
- momentum: float32 [3072, 18432], P(('fsdp', 'replica'), 'tensor'), may hold values from -6 to 6
- probe: bfloat16 [256, 18432], P('fsdp', 'tensor'), may hold values from -0.046875 to 0.046875
Outputs:
- new_params: float32 [3072, 18432], P(('fsdp', 'replica'), 'tensor')
- new_momentum: float32 [3072, 18432], P(('fsdp', 'replica'), 'tensor')
- probe_out: bfloat16 [256, 3072], P('tensor', 'fsdp')
All inputs are finite; a program needn't handle non-finite values.
Results may differ from a plain program's by a relative error of at most 0.014.
Values may be sent and summed in bfloat16 or wider, within the bound.
A program may use at most 128 MiB of HBM per device.

v0:
```python
import functools

import jax
import jax.numpy as jnp
from jax import lax
from jax.experimental import pallas as pl
from jax.experimental.pallas import tpu as pltpu
from jax.sharding import PartitionSpec as P

outer_rate = 0.7
nesterov = 0.9
f32, bf16 = jnp.float32, jnp.bfloat16
MESH = pl.DeviceIdType.MESH

SLOTS = 4


def mean(summed, n):
    return summed * (1.0 / n) if n & (n - 1) == 0 else summed / n


def kernel(sizes, grad, carried, params, momentum, probe, *refs):
    n, n_fsdp, splits, rows, columns, tile, height = sizes
    (
        new_params, new_momentum, probe_out,
        grad_in, carried_in, give, got, part, arrived, own, probes, total,
        half_out, half_in, blocks,
        grad_sem, carried_sem, state_sem,
        give_send, give_recv, part_send, part_recv,
        fetch_send, fetch_recv, share_send, share_recv,
        half_send, half_recv, block_send, block_recv,
    ) = refs
    chips = n // 2
    tiles = columns // tile
    items = chips * tiles
    me = lax.axis_index("replica")
    chip, core = lax.div(me, 2), lax.rem(me, 2)
    here = lax.axis_index("fsdp")
    mine = lax.axis_index("tensor")
    mate = {"replica": chip * 2 + 1 - core}
    across = [{"replica": lax.rem(chip + s, chips) * 2 + core} for s in range(1, chips)]
    along = [{"fsdp": lax.rem(here + s, n_fsdp)} for s in range(1, n_fsdp)]
    beside = [{"tensor": lax.rem(mine + s, splits)} for s in range(1, splits)]

    def remote(src, dst, send, recv, device):
        return pltpu.make_async_remote_copy(
            src_ref=src, dst_ref=dst, send_sem=send, recv_sem=recv,
            device_id=device, device_id_type=MESH,
        )

    def fetch(k):
        there = lax.rem(chip + 1 + lax.div(k, tiles), chips)
        slot = lax.rem(k, SLOTS)
        at = (
            0,
            pl.ds(pl.multiple_of(there * (2 * rows), 2 * rows), 2 * rows),
            pl.ds(pl.multiple_of(lax.rem(k, tiles) * tile, tile), tile),
        )
        return (
            pltpu.make_async_copy(grad.at[at], grad_in.at[slot], grad_sem.at[slot]),
            pltpu.make_async_copy(carried.at[at], carried_in.at[slot], carried_sem.at[slot]),
        )

    def start_fetch(k):
        for copy in fetch(k):
            copy.start()

    def outgoing(k, which):
        slot = lax.rem(k, SLOTS)
        at = pl.ds(pl.multiple_of(which * rows, rows), rows)
        return grad_in[slot, at, :].astype(f32) + carried_in[slot, at, :]

    def give_copy(k):
        slot = lax.rem(k, SLOTS)
        return remote(give.at[slot], got.at[k], give_send.at[slot], give_recv.at[k], mate)

    def part_copy(k, step):
        return remote(part.at[k], arrived.at[k], part_send.at[k], part_recv.at[k], across[step])

    def first(k):
        for copy in fetch(k):
            copy.wait()

        @pl.when(k >= SLOTS)
        def _():
            give_copy(k - SLOTS).wait_send()

        give[lax.rem(k, SLOTS)] = outgoing(k, 1 - core).astype(bf16)
        give_copy(k).start()

    def second(k, step):
        give_copy(k).wait_recv()
        summed = outgoing(k, core) + got[k].astype(f32)
        if step < chips - 1:
            part[k] = summed.astype(bf16)
            part_copy(k, step).start()
        else:
            own[k - step * tiles] = summed

        @pl.when(k + SLOTS < items)
        def _():
            start_fetch(k + SLOTS)

    for k in range(min(SLOTS, items)):
        start_fetch(jnp.int32(k))

    barrier = pltpu.get_barrier_semaphore()
    peers = [mate] + across + along + beside
    for peer in peers:
        pl.semaphore_signal(barrier, inc=1, device_id=peer, device_id_type=MESH)
    pl.semaphore_wait(barrier, len(peers))

    half = height // 2
    half_at = lambda place: pl.ds(pl.multiple_of(place * height + core * half, half), half)
    own_half = pl.ds(pl.multiple_of(core * half, half), half)
    own_probe = pltpu.make_async_copy(
        probe, probes.at[pl.ds(pl.multiple_of(here * height, height), height), :], state_sem.at[2]
    )

    def probe_copy(step):
        return remote(
            probe.at[own_half, :], probes.at[half_at(here), :],
            fetch_send.at[step], fetch_recv.at[step], along[step],
        )

    def share_copy(step):
        place = half_at(lax.rem(here + n_fsdp - 1 - step, n_fsdp))
        return remote(
            probes.at[place, :], probes.at[place, :],
            share_send.at[step], share_recv.at[step], mate,
        )

    first(jnp.int32(0))
    state = (
        pltpu.make_async_copy(params, new_params, state_sem.at[0]),
        pltpu.make_async_copy(momentum, new_momentum, state_sem.at[1]),
    )
    for step in range(chips):
        last = step == chips - 1

        def body(k, carry, step=step):
            first(k)
            second(k - 1, step)
            return carry

        lax.fori_loop(step * tiles + 1, (step + 1) * tiles + (0 if last else 1), body, 0)
        if step == 0:
            own_probe.start()
            for i in range(n_fsdp - 1):
                probe_copy(i).start()
            for copy in state:
                copy.start()
    second(jnp.int32(items - 1), chips - 1)

    for copy in state:
        copy.wait()
    own_probe.wait()
    total[...] = jnp.zeros_like(total)

    def update(t):
        at = pl.ds(pl.multiple_of(t * tile, tile), tile)
        summed = own[t]
        for step in range(chips - 1):
            k = step * tiles + t
            part_copy(k, step).wait_recv()
            summed += arrived[k].astype(f32)
        average = mean(summed, n)
        moved = nesterov * new_momentum[:, at] + average
        updated = new_params[:, at] - outer_rate * (average + nesterov * moved)
        new_momentum[:, at] = moved
        new_params[:, at] = updated
        return updated.astype(bf16)

    def product(t, weights):
        at = pl.ds(pl.multiple_of(t * tile, tile), tile)
        total[...] += lax.dot_general(
            probes[:, at], weights, (((1,), (1,)), ((), ())), preferred_element_type=f32
        )

    early = max(1, (2 * tiles) // 3)

    def before(t, carry):
        got[t] = update(t)
        return carry

    lax.fori_loop(0, early, before, 0)
    for i in range(n_fsdp - 1):
        probe_copy(i).wait_recv()
        share_copy(i).start()
    for i in range(n_fsdp - 1):
        share_copy(i).wait_recv()

    def backlog(t, carry):
        product(t, got[t])
        return carry

    lax.fori_loop(0, early, backlog, 0)

    def after(t, carry):
        product(t, update(t))
        return carry

    lax.fori_loop(early, tiles, after, 0)

    batch = half_out.shape[1]
    piece = lambda which: total[pl.ds(pl.multiple_of(which * batch, batch), batch), :]
    halves = []
    for i in range(splits - 1):
        half_out[i] = piece(lax.rem(mine + 1 + i, splits)).astype(bf16)
        copy = remote(half_out.at[i], half_in.at[i], half_send.at[i], half_recv.at[i], beside[i])
        copy.start()
        halves.append(copy)
    column_part = piece(mine)
    for i, copy in enumerate(halves):
        copy.wait_recv()
        column_part += half_in[i].astype(f32)
    blocks[me] = column_part.astype(bf16)

    def block_copy(which, slot, device):
        return remote(
            blocks.at[which], blocks.at[which], block_send.at[slot], block_recv.at[slot], device
        )

    sends = [block_copy(me, s, across[s]) for s in range(chips - 1)]
    sends.append(block_copy(me, chips - 1, mate))
    for copy in sends:
        copy.start()
    for s in range(chips - 1):
        source = lax.rem(chip + chips - 1 - s, chips) * 2 + core
        sends[s].wait_recv()
        copy = block_copy(source, chips + s, mate)
        copy.start()
        sends.append(copy)
    for copy in sends[chips - 1 :]:
        copy.wait_recv()
    probe_out[...] = jnp.concatenate([blocks[r] for r in range(n)], axis=1)

    for copy in halves + sends:
        copy.wait_send()
    for k in range(max(0, items - SLOTS), items):
        give_copy(jnp.int32(k)).wait_send()
    for step in range(chips - 1):
        def drain(k, carry, step=step):
            part_copy(k, step).wait_send()
            return carry

        lax.fori_loop(step * tiles, (step + 1) * tiles, drain, 0)
    for i in range(n_fsdp - 1):
        probe_copy(i).wait_send()
        share_copy(i).wait_send()


def per_device(pseudo_grad, compensation, params, momentum, probe):
    n = lax.axis_size("replica")
    n_fsdp = lax.axis_size("fsdp")
    splits = lax.axis_size("tensor")
    chips = n // 2
    rows, columns = params.shape
    height = probe.shape[0]
    tile = 512 if columns % 512 == 0 else 128
    tiles = columns // tile
    batch = n_fsdp * height
    dma = pltpu.SemaphoreType.DMA
    anywhere = pl.BlockSpec(memory_space=pl.ANY)
    vmem = pl.BlockSpec(memory_space=pltpu.VMEM)
    links = max(1, n_fsdp - 1)
    return pl.pallas_call(
        functools.partial(kernel, (n, n_fsdp, splits, rows, columns, tile, height)),
        out_shape=(
            pltpu.VMEM((rows, columns), f32),
            pltpu.VMEM((rows, columns), f32),
            jax.ShapeDtypeStruct((batch // splits, n * rows), bf16),
        ),
        in_specs=[anywhere] * 5,
        out_specs=[vmem] * 3,
        scratch_shapes=[
            pltpu.VMEM((SLOTS, 2 * rows, tile), bf16),
            pltpu.VMEM((SLOTS, 2 * rows, tile), f32),
            pltpu.VMEM((SLOTS, rows, tile), bf16),
            pltpu.VMEM((chips * tiles, rows, tile), bf16),
            pltpu.VMEM(((chips - 1) * tiles, rows, tile), bf16),
            pltpu.VMEM(((chips - 1) * tiles, rows, tile), bf16),
            pltpu.VMEM((tiles, rows, tile), f32),
            pltpu.VMEM((batch, columns), bf16),
            pltpu.VMEM((batch, rows), f32),
            pltpu.VMEM((splits - 1, batch // splits, rows), bf16),
            pltpu.VMEM((splits - 1, batch // splits, rows), bf16),
            pltpu.VMEM((n, batch // splits, rows), bf16),
            dma((SLOTS,)), dma((SLOTS,)), dma((3,)),
            dma((SLOTS,)), dma((chips * tiles,)),
            dma(((chips - 1) * tiles,)), dma(((chips - 1) * tiles,)),
            dma((links,)), dma((links,)), dma((links,)), dma((links,)),
            dma((splits - 1,)), dma((splits - 1,)),
            dma((n - 1,)), dma((n - 1,)),
        ],
        compiler_params=pltpu.CompilerParams(
            collective_id=0, has_side_effects=True, vmem_limit_bytes=46 * 1024 * 1024
        ),
    )(pseudo_grad, compensation, params, momentum, probe)


def solution(mesh):
    in_specs = (
        P("replica", "fsdp", "tensor"),
        P("replica", "fsdp", "tensor"),
        P(("fsdp", "replica"), "tensor"),
        P(("fsdp", "replica"), "tensor"),
        P("fsdp", "tensor"),
    )
    out_specs = (
        P(("fsdp", "replica"), "tensor"),
        P(("fsdp", "replica"), "tensor"),
        P("tensor", "fsdp"),
    )
    return jax.shard_map(
        per_device, mesh=mesh, in_specs=in_specs, out_specs=out_specs, check_vma=False
    )
```

profile of v0, /device:TPU:0, one launch (start us, length us, event | category | flops | bytes accessed | tf_op | source)
XLA Modules:
  0.0 101.2 jit_solution(11001374778424926631)
XLA Ops:
  0.6 94.0 %shard_map.76 = (f32[192,9216]{1,0:T(8,128)S(1)}, f32[192,9216]{1,0:T(8,128)S(1)}, bf16[128,768]{1,0:T(8,128)(2,1)}) custom-call(bf16[1,768,9216]{2,1,0:T(8,128)(2,1)} %grad.1, f32[1,768,9216]{2,1,0:T(8,128)} %carried.1, f32[192,9216]{1,0:T(8,128)} %params.1, f32[192,9216]{1,0:T(8,128)} %momentum.1, bf16[64,9216]{1,0:T(8,128)(2,1)} %probe.1), custom_call_target="tpu_custom_call" | custom-call | tf_op jit(solution)/shard_map/pallas_call | solution.py:267
  94.6 3.0 %copy.11 = f32[192,9216]{1,0:T(8,128)} copy(f32[192,9216]{1,0:T(8,128)S(1)} %get-tuple-element.3) | data formatting | bytes 14155776
  97.6 0.0 copy-start
  97.6 3.0 %copy.12 = f32[192,9216]{1,0:T(8,128)} copy(f32[192,9216]{1,0:T(8,128)S(1)} %get-tuple-element.4) | data formatting | bytes 14155776
  100.5 0.0 copy-done
  100.5 0.7 copy.13
Async XLA Ops:
  97.6 3.0 %copy-start = (bf16[128,768]{1,0:T(8,128)(2,1)S(1)}, bf16[128,768]{1,0:T(8,128)(2,1)}, u32[]{:S(2)}) copy-start(bf16[128,768]{1,0:T(8,128)(2,1)} %get-tuple-element.11) | copy-start | bytes 589828
where the time goes:
time: 102 us; the launch traced here: 101 us
  Pallas kernels  94 us (92%)
  local copies, waits for them, and re-layouts  6.61 us (6%)
    pallas_call x1, Pallas kernels, per_device(): pl.pallas_call(functools.partial(kernel, (n, n_fsdp, splits, rows, column...  94 us
    unnamed x5, local copies, waits for them, and re-layouts  6.61 us

commit v1 on v0

v1 whole, which is shorter than its diff:
```python
import functools

import jax
import jax.numpy as jnp
from jax import lax
from jax.experimental import pallas as pl
from jax.experimental.pallas import tpu as pltpu
from jax.sharding import PartitionSpec as P

outer_rate = 0.7
nesterov = 0.9
f32, bf16 = jnp.float32, jnp.bfloat16
MESH = pl.DeviceIdType.MESH

SLOTS = 4
AHEAD = 6
OPENING = 2
BUFFERS = 11


def mean(summed, n):
    return summed * (1.0 / n) if n & (n - 1) == 0 else summed / n


def segments_of(rows, columns):
    fit = lambda width: width if columns % width == 0 else 128
    late = 32 if rows >= 64 else rows
    if late == rows:
        return [(0, rows, fit(512))]
    return [(0, rows - late, fit(1024)), (rows - late, late, fit(1024))]


def kernel(sizes, grad, carried, params, momentum, probe, *refs):
    n, n_fsdp, splits, rows, columns, height, segments = sizes
    refs = list(refs)
    take = lambda count: [refs.pop(0) for _ in range(count)]
    new_params, new_momentum, gathered = take(3)
    buffers = [take(BUFFERS) for _ in segments]
    probes, late_out, late_in = take(3)
    early_out, early_in = take(2) if len(segments) > 1 else (None, None)
    (
        state_sem, right_send, left_send, fetch_recv, share_send, share_recv,
        late_send, late_recv, early_send, early_recv, block_send, block_recv,
    ) = refs
    chips = n // 2
    me = lax.axis_index("replica")
    chip, core = lax.div(me, 2), lax.rem(me, 2)
    here = lax.axis_index("fsdp")
    mine = lax.axis_index("tensor")
    mate = {"replica": chip * 2 + 1 - core}
    across = [{"replica": lax.rem(chip + s, chips) * 2 + core} for s in range(1, chips)]
    beside = [{"tensor": lax.rem(mine + s, splits)} for s in range(1, splits)]
    multiple = lambda index, size: pl.ds(pl.multiple_of(index * size, size), size)

    def remote(src, dst, send, recv, device):
        return pltpu.make_async_remote_copy(
            src_ref=src, dst_ref=dst, send_sem=send, recv_sem=recv,
            device_id=device, device_id_type=MESH,
        )

    class Segment:
        def __init__(self, spec, parts, held):
            self.row, self.rows, self.tile = spec
            (
                self.grad_in, self.carried_in, self.give, self.got, self.part, self.arrived, self.own,
                self.total, self.in_sem, self.give_sem, self.part_sem,
            ) = parts
            self.tiles = columns // self.tile
            self.items = chips * self.tiles
            self.held = held

        def fetch(self, k):
            there = lax.rem(chip + 1 + lax.div(k, self.tiles), chips)
            slot = lax.rem(k, SLOTS)
            copies = []
            for which in range(2):
                start = (there * 2 + which) * rows + self.row
                at = (0, pl.ds(pl.multiple_of(start, 16), self.rows), multiple(lax.rem(k, self.tiles), self.tile))
                for i, (array, into) in enumerate(((grad, self.grad_in), (carried, self.carried_in))):
                    copies.append(
                        pltpu.make_async_copy(
                            array.at[at], into.at[slot, which], self.in_sem.at[slot, 2 * which + i]
                        )
                    )
            return copies

        def start_fetch(self, k):
            for copy in self.fetch(k):
                copy.start()

        def outgoing(self, k, which):
            slot = lax.rem(k, SLOTS)
            return self.grad_in[slot, which].astype(f32) + self.carried_in[slot, which]

        def give_copy(self, k):
            slot = lax.rem(k, SLOTS)
            return remote(self.give.at[slot], self.got.at[k], self.give_sem.at[slot], self.give_sem.at[SLOTS + k], mate)

        def part_copy(self, k, step):
            return remote(
                self.part.at[k], self.arrived.at[k], self.part_sem.at[0, k], self.part_sem.at[1, k], across[step]
            )

        def first(self, k, send=True):
            for copy in self.fetch(k):
                copy.wait()

            @pl.when(k >= SLOTS)
            def _():
                self.give_copy(k - SLOTS).wait_send()

            self.give[lax.rem(k, SLOTS)] = self.outgoing(k, 1 - core).astype(bf16)
            if send:
                self.give_copy(k).start()

        def second(self, k, step, now=False):
            summed = self.outgoing(k, core)
            self.give_copy(k).wait_recv()
            summed += self.got[k].astype(f32)
            if step < chips - 1:
                self.part[k] = summed.astype(bf16)
                if now or not self.held:
                    self.part_copy(k, step).start()
            else:
                self.own[k - step * self.tiles] = summed

            @pl.when(k + SLOTS < self.items)
            def _():
                self.start_fetch(k + SLOTS)

        def run(self, step, begun=0):
            start, end = step * self.tiles + begun, (step + 1) * self.tiles
            if start >= end:
                return
            self.first(jnp.int32(start))

            def body(k, carry):
                self.first(k)
                self.second(k - 1, step)
                return carry

            lax.fori_loop(start + 1, end, body, 0)
            self.second(jnp.int32(end - 1), step)

        def update(self, t):
            at = (pl.ds(self.row, self.rows), multiple(t, self.tile))
            summed = self.own[t]
            for step in range(chips - 1):
                k = step * self.tiles + t
                self.part_copy(k, step).wait_recv()
                summed += self.arrived[k].astype(f32)
            average = mean(summed, n)
            moved = nesterov * new_momentum[at] + average
            updated = new_params[at] - outer_rate * (average + nesterov * moved)
            new_momentum[at] = moved
            new_params[at] = updated
            return updated.astype(bf16)

        def product(self, t, weights):
            self.total[...] += lax.dot_general(
                weights, probes[:, multiple(t, self.tile)], (((1,), (1,)), ((), ())),
                preferred_element_type=f32,
            )

        def drain(self):
            for k in range(max(0, self.items - SLOTS), self.items):
                self.give_copy(jnp.int32(k)).wait_send()
            for step in range(chips - 1):
                def body(k, carry, step=step):
                    self.part_copy(k, step).wait_send()
                    return carry

                lax.fori_loop(step * self.tiles, (step + 1) * self.tiles, body, 0)

    held = len(segments) > 1 and chips == 2
    parts = [Segment(s, b, held and i == 1) for i, (s, b) in enumerate(zip(segments, buffers))]
    main, late = parts[0], parts[-1]

    for k in range(min(OPENING, late.tiles)):
        late.start_fetch(jnp.int32(k))
    barrier = pltpu.get_barrier_semaphore()
    others = [(r, t) for r in range(n) for t in range(splits) if r or t]
    other = lambda r, t: {"replica": lax.rem(me + r, n), "tensor": lax.rem(mine + t, splits)}
    near = [mate] + across + beside if len(segments) > 1 else [other(r, t) for r, t in others]
    for peer in near:
        pl.semaphore_signal(barrier, inc=1, device_id=peer, device_id_type=MESH)
    is_right, is_left = here + 1 < n_fsdp, here >= 1
    right, left = {"fsdp": here + 1}, {"fsdp": here - 1}

    @pl.when(is_right)
    def _():
        pl.semaphore_signal(barrier, inc=1, device_id=right, device_id_type=MESH)

    @pl.when(is_left)
    def _():
        pl.semaphore_signal(barrier, inc=1, device_id=left, device_id_type=MESH)

    opening = min(OPENING, late.tiles)
    late.first(jnp.int32(0), send=False)
    if main is not late:
        main.start_fetch(jnp.int32(0))
    pl.semaphore_wait(barrier, len(near) + is_right.astype(jnp.int32) + is_left.astype(jnp.int32))

    half = height // 2
    half_at = lambda place: pl.ds(pl.multiple_of(place * height + core * half, half), half)
    own_probe = pltpu.make_async_copy(probe, probes.at[multiple(here, height), :], state_sem.at[2])

    def right_copy(s):
        block = here - s + 1
        src = probe.at[multiple(core, half), :] if s == 1 else probes.at[half_at(block), :]
        return remote(src, probes.at[half_at(block), :], right_send.at[s - 1], fetch_recv.at[block], right)

    def left_copy(s):
        block = here + s - 1
        src = probe.at[multiple(core, half), :] if s == 1 else probes.at[half_at(block), :]
        return remote(src, probes.at[half_at(block), :], left_send.at[s - 1], fetch_recv.at[block], left)

    def share_copy(block):
        place = half_at(block)
        return remote(probes.at[place, :], probes.at[place, :], share_send.at[block], share_recv.at[block], mate)

    def relay(s, act):
        @pl.when(is_right & (here - s + 1 >= 0))
        def _():
            act(right_copy(s))

        @pl.when(is_left & (here + s - 1 < n_fsdp))
        def _():
            act(left_copy(s))

    start = lambda copy: copy.start()
    wait_send = lambda copy: copy.wait_send()
    wait_recv = lambda copy: copy.wait_recv()

    def landed(s, act):
        @pl.when(here - s >= 0)
        def _():
            act(here - s, right_copy)

        @pl.when(here + s < n_fsdp)
        def _():
            act(here + s, left_copy)

    def land(s):
        def act(block, _):
            place = half_at(block)
            remote(
                probes.at[place, :], probes.at[place, :], right_send.at[0], fetch_recv.at[block], mate
            ).wait_recv()
            share_copy(block).start()

        landed(s, act)
        if s + 1 < n_fsdp:
            relay(s + 1, start)

    late.give_copy(jnp.int32(0)).start()
    for k in range(1, opening):
        late.first(jnp.int32(k))
    for k in range(opening):
        late.second(jnp.int32(k), 0, now=True)
    if n_fsdp > 1:
        relay(1, start)
    own_probe.start()
    if main is not late:
        for k in range(1, min(SLOTS, main.items)):
            main.start_fetch(jnp.int32(k))
    for k in range(opening, min(SLOTS, late.items)):
        late.start_fetch(jnp.int32(k))
    state = (
        pltpu.make_async_copy(params, new_params, state_sem.at[0]),
        pltpu.make_async_copy(momentum, new_momentum, state_sem.at[1]),
    )
    for step in range(chips - 1):
        for i, part in enumerate(parts):
            part.run(step, begun=opening if step == 0 and part is late else 0)
    for copy in state:
        copy.start()
    if n_fsdp > 1:
        land(1)
    for part in parts:
        part.run(chips - 1)
    if n_fsdp > 2:
        land(2)
    for copy in state:
        copy.wait()
    own_probe.wait()
    for part in parts:
        part.total[...] = jnp.zeros_like(part.total)

    first_products = max(1, (2 * main.tiles) // 3)

    def before(t, carry):
        main.got[t] = main.update(t)
        return carry

    lax.fori_loop(0, first_products, before, 0)
    for s in range(3, n_fsdp):
        land(s)
    for s in range(1, n_fsdp):
        landed(s, lambda block, _: share_copy(block).wait_recv())

    def backlog(t, carry):
        main.product(t, main.got[t])
        return carry

    lax.fori_loop(0, first_products, backlog, 0)

    def after(part):
        def body(t, carry):
            part.product(t, part.update(t))
            return carry

        return body

    batch = n_fsdp * height
    piece = batch // splits
    copies = []
    if len(parts) == 1:
        lax.fori_loop(first_products, main.tiles, after(main), 0)
    else:
        turn = max(first_products, main.tiles - 2)
        lax.fori_loop(first_products, turn, after(main), 0)
        lead = min(AHEAD, late.tiles - opening)
        if held:
            for k in range(opening, opening + lead):
                late.part_copy(jnp.int32(k), 0).start()
        lax.fori_loop(turn, main.tiles, after(main), 0)

        halves = []
        for i in range(splits - 1):
            early_out[i] = main.total[:, multiple(lax.rem(mine + 1 + i, splits), piece)].astype(bf16)
            copy = remote(early_out.at[i], early_in.at[i], early_send.at[i], early_recv.at[i], beside[i])
            copy.start()
            halves.append(copy)
        copies += halves

        def late_step(t, carry):
            if held:
                @pl.when(t + opening + lead < late.tiles)
                def _():
                    late.part_copy(t + opening + lead, 0).start()

            return after(late)(t, carry)

        middle = min(3, late.tiles)
        lax.fori_loop(0, middle, late_step, 0)
        summed = main.total[:, multiple(mine, piece)]
        for i, copy in enumerate(halves):
            copy.wait_recv()
            summed += early_in[i].astype(f32)
        block_at = lambda which: pl.ds(pl.multiple_of(which * rows, 16), main.rows)
        gathered[block_at(me), :] = summed.astype(bf16)

        def block_copy(which, slot, device):
            ref = gathered.at[block_at(which), :]
            return remote(ref, ref, block_send.at[slot], block_recv.at[slot], device)

        sends = [block_copy(me, s, across[s]) for s in range(chips - 1)]
        sends.append(block_copy(me, chips - 1, mate))
        for copy in sends:
            copy.start()
        lax.fori_loop(middle, late.tiles, late_step, 0)

    for t in range(splits):
        late_out[t] = late.total[:, multiple(lax.rem(mine + t, splits), piece)].astype(bf16)
    messages = [
        remote(
            late_out.at[t], late_in.at[r * splits + t],
            late_send.at[r * splits + t], late_recv.at[r * splits + t], other(r, t),
        )
        for r, t in others
    ]
    for copy in messages:
        copy.start()
    copies += messages
    if len(parts) > 1:
        for s in range(chips - 1):
            source = lax.rem(chip + chips - 1 - s, chips) * 2 + core
            sends[s].wait_recv()
            copy = block_copy(source, chips + s, mate)
            copy.start()
            sends.append(copy)
        copies += sends
    for part in parts:
        part.drain()
    for s in range(1, n_fsdp):
        relay(s, wait_send)
        landed(s, lambda block, _: share_copy(block).wait_send())
    for copy in messages:
        copy.wait_recv()
    for r in range(n):
        summed = jnp.zeros((late.rows, piece), f32)
        for t in range(splits):
            summed += (late_in[r * splits + t] if r or t else late_out[0]).astype(f32)
        source = lax.rem(me + n - r, n)
        gathered[pl.ds(pl.multiple_of(source * rows + late.row, 16), late.rows), :] = summed.astype(bf16)
    if len(parts) > 1:
        for copy in sends[chips - 1 :]:
            copy.wait_recv()
    for copy in copies:
        copy.wait_send()


def writer(params_in, momentum_in, gathered, params_out, momentum_out, probe_out, turned, sem):
    copies = (
        pltpu.make_async_copy(params_in, params_out, sem.at[0]),
        pltpu.make_async_copy(momentum_in, momentum_out, sem.at[1]),
    )
    for copy in copies:
        copy.start()
    turned[...] = gathered[...].astype(f32).T.astype(bf16)
    last = pltpu.make_async_copy(turned, probe_out, sem.at[2])
    last.start()
    for copy in (*copies, last):
        copy.wait()


def per_device(pseudo_grad, compensation, params, momentum, probe):
    n = lax.axis_size("replica")
    n_fsdp = lax.axis_size("fsdp")
    splits = lax.axis_size("tensor")
    chips = n // 2
    rows, columns = params.shape
    height = probe.shape[0]
    batch = n_fsdp * height
    piece = batch // splits
    segments = segments_of(rows, columns)
    dma = pltpu.SemaphoreType.DMA
    anywhere = pl.BlockSpec(memory_space=pl.ANY)
    vmem = pl.BlockSpec(memory_space=pltpu.VMEM)
    scratch = []
    for _, high, tile in segments:
        tiles = columns // tile
        sends = max(1, chips - 1) * tiles
        scratch += [
            pltpu.VMEM((SLOTS, 2, high, tile), bf16),
            pltpu.VMEM((SLOTS, 2, high, tile), f32),
            pltpu.VMEM((SLOTS, high, tile), bf16),
            pltpu.VMEM((chips * tiles, high, tile), bf16),
            pltpu.VMEM((sends, high, tile), bf16),
            pltpu.VMEM((sends, high, tile), bf16),
            pltpu.VMEM((tiles, high, tile), f32),
            pltpu.VMEM((high, batch), f32),
            dma((SLOTS, 4)),
            dma((SLOTS + chips * tiles,)),
            dma((2, sends)),
        ]
    _, late, _ = segments[-1]
    early = segments[0][1]
    scratch += [
        pltpu.VMEM((batch, columns), bf16),
        pltpu.VMEM((splits, late, piece), bf16),
        pltpu.VMEM((n * splits, late, piece), bf16),
    ]
    if len(segments) > 1:
        scratch += [pltpu.VMEM((max(1, splits - 1), early, piece), bf16)] * 2
    links = max(1, n_fsdp)
    scratch += [dma((3,))] + [dma((links,))] * 5 + [dma((n * splits,))] * 2 + [dma((splits,))] * 2 + [dma((n,))] * 2
    full = pltpu.VMEM((rows, columns), f32)
    new_params, new_momentum, gathered = pl.pallas_call(
        functools.partial(kernel, (n, n_fsdp, splits, rows, columns, height, segments)),
        out_shape=(full, full, pltpu.VMEM((n * rows, piece), bf16)),
        in_specs=[anywhere] * 5,
        out_specs=[vmem] * 3,
        scratch_shapes=scratch,
        compiler_params=pltpu.CompilerParams(
            collective_id=0, has_side_effects=True, vmem_limit_bytes=46 * 1024 * 1024
        ),
    )(pseudo_grad, compensation, params, momentum, probe)
    full = jax.ShapeDtypeStruct((rows, columns), f32)
    return pl.pallas_call(
        writer,
        out_shape=(full, full, jax.ShapeDtypeStruct((piece, n * rows), bf16)),
        in_specs=[vmem] * 3,
        out_specs=[anywhere] * 3,
        scratch_shapes=[pltpu.VMEM((piece, n * rows), bf16), dma((3,))],
        compiler_params=pltpu.CompilerParams(vmem_limit_bytes=8 * 1024 * 1024),
    )(*(pltpu.with_memory_space_constraint(x, pltpu.VMEM) for x in (new_params, new_momentum, gathered)))


def solution(mesh):
    in_specs = (
        P("replica", "fsdp", "tensor"),
        P("replica", "fsdp", "tensor"),
        P(("fsdp", "replica"), "tensor"),
        P(("fsdp", "replica"), "tensor"),
        P("fsdp", "tensor"),
    )
    out_specs = (
        P(("fsdp", "replica"), "tensor"),
        P(("fsdp", "replica"), "tensor"),
        P("tensor", "fsdp"),
    )
    return jax.shard_map(
        per_device, mesh=mesh, in_specs=in_specs, out_specs=out_specs, check_vma=False
    )
```

time: 102 us -> 93.6 us (0.918)
  local copies, waits for them, and re-layouts: 6.61 us -> 0 us
  Pallas kernels: 94 us -> 92.7 us
    pallas_call x1, Pallas kernels: 94 us -> 87.4 us  [per_device(): pl.pallas_call(functools.partial(kernel, (n, n_fsdp, splits, rows, column...]
    unnamed x5 -> x0, local copies, waits for them, and re-layouts: 6.61 us -> none
    pallas_call x0 -> x1, Pallas kernels: none -> 5.32 us  [per_device(): pl.pallas_call(writer, out_shape=(full, full, jax.ShapeDtypeStruct((piece...]
where the time goes in v1:
time: 93.6 us; the launch traced here: 93.3 us
  Pallas kernels  92.7 us (99%)
    pallas_call x1, Pallas kernels, per_device(): pl.pallas_call(functools.partial(kernel, (n, n_fsdp, splits, rows, column...  87.4 us
    pallas_call x1, Pallas kernels, per_device(): pl.pallas_call(writer, out_shape=(full, full, jax.ShapeDtypeStruct((piece...  5.32 us

profile of v1, /device:TPU:0, one launch (start us, length us, event | category | flops | bytes accessed | tf_op | source)
XLA Modules:
  0.0 93.3 jit_solution(17511165575514322735)
XLA Ops:
  0.6 87.4 %shard_map.76 = (f32[192,9216]{1,0:T(8,128)S(1)}, f32[192,9216]{1,0:T(8,128)S(1)}, bf16[768,128]{1,0:T(8,128)(2,1)S(1)}) custom-call(bf16[1,768,9216]{2,1,0:T(8,128)(2,1)} %grad.1, f32[1,768,9216]{2,1,0:T(8,128)} %carried.1, f32[192,9216]{1,0:T(8,128)} %params.1, f32[192,9216]{1,0:T(8,128)} %momentum.1, bf16[64,9216]{1,0:T(8,128)(2,1)} %probe.1), custom_call_target="tpu_custom_call" | custom-call | tf_op jit(solution)/shard_map/pallas_call | solution.py:460
  88.0 5.3 %shard_map.77 = (f32[192,9216]{1,0:T(8,128)}, f32[192,9216]{1,0:T(8,128)}, bf16[128,768]{1,0:T(8,128)(2,1)}) custom-call(f32[192,9216]{1,0:T(8,128)S(1)} %get-tuple-element.6.params_in, f32[192,9216]{1,0:T(8,128)S(1)} %get-tuple-element.7.momentum_in, bf16[768,128]{1,0:T(8,128)(2,1)S(1)} %get-tuple-element.8.gathered), custom_call_target="tpu_custom_call" | custom-call | tf_op jit(solution)/shard_map/pallas_call | solution.py:471

commit v2 on v1

--- a/solution.py
+++ b/solution.py
@@ -12,9 +12,9 @@
 f32, bf16 = jnp.float32, jnp.bfloat16
 MESH = pl.DeviceIdType.MESH
 
-SLOTS = 4
+SLOTS = 3
 AHEAD = 6
-OPENING = 2
+OPENING = 3
 BUFFERS = 11
 
 
@@ -27,7 +27,7 @@
     late = 32 if rows >= 64 else rows
     if late == rows:
         return [(0, rows, fit(512))]
-    return [(0, rows - late, fit(1024)), (rows - late, late, fit(1024))]
+    return [(0, rows - late, fit(1536)), (rows - late, late, fit(1024))]
 
 
 def kernel(sizes, grad, carried, params, momentum, probe, *refs):
@@ -402,12 +402,12 @@
 
 
 def writer(params_in, momentum_in, gathered, params_out, momentum_out, probe_out, turned, sem):
-    copies = (
+    copies = [
         pltpu.make_async_copy(params_in, params_out, sem.at[0]),
         pltpu.make_async_copy(momentum_in, momentum_out, sem.at[1]),
-    )
-    for copy in copies:
-        copy.start()
+    ]
+    for priority, copy in enumerate(copies):
+        copy.start(priority=priority)
     turned[...] = gathered[...].astype(f32).T.astype(bf16)
     last = pltpu.make_async_copy(turned, probe_out, sem.at[2])
     last.start()

time: 93.6 us -> 93.5 us (level)
  no operation moved by 1% of the time
where the time goes in v2:
time: 93.5 us; the launch traced here: 93.2 us
  Pallas kernels  92.5 us (99%)
    pallas_call x1, Pallas kernels, per_device(): pl.pallas_call(functools.partial(kernel, (n, n_fsdp, splits, rows, column...  87.2 us
    pallas_call x1, Pallas kernels, per_device(): pl.pallas_call(writer, out_shape=(full, full, jax.ShapeDtypeStruct((piece...  5.38 us

profile of v2, /device:TPU:0, one launch (start us, length us, event | category | flops | bytes accessed | tf_op | source)
XLA Modules:
  0.0 93.2 jit_solution(2967297985012808301)
XLA Ops:
  0.6 87.2 %shard_map.76 = (f32[192,9216]{1,0:T(8,128)S(1)}, f32[192,9216]{1,0:T(8,128)S(1)}, bf16[768,128]{1,0:T(8,128)(2,1)S(1)}) custom-call(bf16[1,768,9216]{2,1,0:T(8,128)(2,1)} %grad.1, f32[1,768,9216]{2,1,0:T(8,128)} %carried.1, f32[192,9216]{1,0:T(8,128)} %params.1, f32[192,9216]{1,0:T(8,128)} %momentum.1, bf16[64,9216]{1,0:T(8,128)(2,1)} %probe.1), custom_call_target="tpu_custom_call" | custom-call | tf_op jit(solution)/shard_map/pallas_call | solution.py:460
  87.8 5.4 %shard_map.77 = (f32[192,9216]{1,0:T(8,128)}, f32[192,9216]{1,0:T(8,128)}, bf16[128,768]{1,0:T(8,128)(2,1)}) custom-call(f32[192,9216]{1,0:T(8,128)S(1)} %get-tuple-element.6.params_in, f32[192,9216]{1,0:T(8,128)S(1)} %get-tuple-element.7.momentum_in, bf16[768,128]{1,0:T(8,128)(2,1)S(1)} %get-tuple-element.8.gathered), custom_call_target="tpu_custom_call" | custom-call | tf_op jit(solution)/shard_map/pallas_call | solution.py:471
